TPU v7x, 32 devices: a whole 2x2x4 slice. The times are simulated.
32 devices in a mesh: pair: 8 (over z, y), occ: 4 (over x, core).
Axes of the slice: x: 2, y: 2, z: 4, core: 2. Of those that a mesh axis runs over, the one named last changes fastest.
Arguments:
- amplitudes: float32 [64, 128, 128], P('pair'), may hold values from -4 to 4
- exchange_ints: float32 [64, 128, 128], P('pair'), may hold values from -6 to 6
- pno_energy: float32 [64, 128], P('pair'), may hold values from 0.3 to 3
- pair_shift: float32 [64], P('pair'), may hold values from 0.5 to 2
- coefficients: bfloat16 [64, 512, 128], P('pair'), may hold values from -0.5 to 0.5
- domain_tiles: int32 [64, 4], P('pair'), may hold values from 0 to 3, each once within a row
- couple_owner: int32 [4, 64, 2, 1], P('occ', 'pair'), may hold values from 0 to 7; in each aligned block of 16 rows (0 to 15, 16 to 31, ..., all dimensions but the last counted through in order) at most 3 rows name the same one
- couple_index: int32 [4, 64, 2], P('occ', 'pair'), may hold values from 0 to 7
- couple_weight: float32 [4, 64, 2], P('occ', 'pair'), may hold values from -0.5 to 0.5
Outputs:
- final_amplitudes: float32 [64, 128, 128], P('pair')
- final_residual: float32 [64, 128, 128], P('pair')
Inputs may be any that keep to these rules, and one draw needn't show every extreme that they name: `couple_owner`: among the couplings held by one device (one block of 16 entries), no owner is named more than 3 times. `domain_tiles`: the tiles of one pair's domain are distinct.
All inputs are finite; a program needn't handle non-finite values.
Results may differ from a plain program's by a relative error of at most 0.0003.
Values may be sent and summed in bfloat16 or wider, within the bound.
No kernel may reach another device: no remote copies, remote signals or barrier semaphores. Data moves between devices by JAX's collectives and lax.ppermute only.
A program may use at most 128 MiB of HBM per device.

v0:
```python
import jax
import jax.numpy as jnp
from jax import lax
from jax.sharding import PartitionSpec as P

ITERS = 2


HIGHEST = lax.Precision.HIGHEST


def local(
    amplitudes,
    exchange_ints,
    pno_energy,
    pair_shift,
    coefficients,
    domain_tiles,
    couple_owner,
    couple_index,
    couple_weight,
):
    pair_count = amplitudes.shape[0]
    pno_width = amplitudes.shape[1]
    domain = coefficients.shape[1]
    tile_count = domain_tiles.shape[1]
    couple_count = couple_index.shape[2]
    peer_count = lax.axis_size("pair")
    owners = couple_owner.reshape(-1)
    local_index = couple_index.reshape(-1)
    weights = couple_weight.reshape(pair_count, couple_count)
    total_count = owners.shape[0]
    capacity = max(2, 3 * total_count // (2 * peer_count))
    slot_total = peer_count * capacity
    position = jnp.arange(total_count, dtype=jnp.int32)
    same_owner = (owners[:, None] == owners[None, :]) & (position[None, :] < position[:, None])
    slot_rank = jnp.sum(same_owner.astype(jnp.int32), axis=1)
    slot_ids = owners * capacity + slot_rank
    requester_tiles = jnp.repeat(domain_tiles, couple_count, axis=0)
    payload = jnp.concatenate([local_index[:, None], requester_tiles], axis=1)
    requests = jnp.full((slot_total, 1 + tile_count), -1, jnp.int32).at[slot_ids].set(payload)
    arrived = lax.all_to_all(requests, "pair", split_axis=0, concat_axis=0, tiled=True)
    wanted = arrived[:, 0]
    their_tiles = arrived[:, 1:]
    pick_pair = wanted[:, None] == jnp.arange(pair_count, dtype=jnp.int32)[None, :]
    tile_match = their_tiles[:, :, None, None] == domain_tiles[None, None, :, :]
    selector = (pick_pair[:, None, :, None] & tile_match).astype(jnp.bfloat16)
    selector = selector.reshape(slot_total * tile_count, pair_count * tile_count)
    tile_blocks = coefficients.reshape(pair_count * tile_count, domain // tile_count * pno_width)
    moved_tiles = jnp.dot(selector, tile_blocks, preferred_element_type=jnp.float32).astype(
        jnp.bfloat16
    )
    moved_tiles = moved_tiles.reshape(slot_total, domain, pno_width)
    returned = lax.all_to_all(moved_tiles, "pair", split_axis=0, concat_axis=0, tiled=True)
    their_coef = jnp.take(returned, slot_ids, axis=0).reshape(
        pair_count, couple_count, domain, pno_width
    )
    intersection = jnp.einsum(
        "pfa,pcfb->pcab", coefficients, their_coef, preferred_element_type=jnp.float32
    )
    denominator = pno_energy[:, :, None] + pno_energy[:, None, :] + pair_shift[:, None, None]
    current = amplitudes
    residual = amplitudes
    for iteration in range(ITERS):
        valid = (wanted >= 0).astype(jnp.float32)[:, None, None]
        packed = jnp.take(current, jnp.clip(wanted, 0, pair_count - 1), axis=0) * valid
        returned_amps = lax.all_to_all(packed, "pair", split_axis=0, concat_axis=0, tiled=True)
        partner_amp = jnp.take(returned_amps, slot_ids, axis=0)
        partner_amp = partner_amp.reshape(pair_count, couple_count, pno_width, pno_width)
        inner_prod = jnp.einsum("pcab,pcbd->pcad", intersection, partner_amp, precision=HIGHEST)
        outer_prod = jnp.einsum("pcad,pced->pcae", inner_prod, intersection, precision=HIGHEST)
        partial_value = jnp.einsum("pc,pcae->pae", weights, outer_prod, precision=HIGHEST)
        shared_sum = lax.psum_scatter(partial_value, "occ", scatter_dimension=1, tiled=True)
        row_count = shared_sum.shape[1]
        row_start = lax.axis_index("occ") * row_count
        ints_part = lax.dynamic_slice_in_dim(exchange_ints, row_start, row_count, 1)
        denom_part = lax.dynamic_slice_in_dim(denominator, row_start, row_count, 1)
        current_part = lax.dynamic_slice_in_dim(current, row_start, row_count, 1)
        residual_part = ints_part + denom_part * current_part - shared_sum
        updated_part = current_part - residual_part / denom_part
        current, residual = (
            lax.all_gather(updated_part, "occ", axis=1, tiled=True),
            lax.all_gather(residual_part, "occ", axis=1, tiled=True),
        )
    return (current, residual)


def solution(mesh):
    in_specs = (
        P("pair", None, None),
        P("pair", None, None),
        P("pair", None),
        P("pair"),
        P("pair", None, None),
        P("pair", None),
        P("occ", "pair", None, None),
        P("occ", "pair", None),
        P("occ", "pair", None),
    )
    out_specs = (P("pair", None, None), P("pair", None, None))
    return jax.shard_map(local, mesh=mesh, in_specs=in_specs, out_specs=out_specs, check_vma=False)
```

profile of v0, /device:TPU:0, one launch (start us, length us, event | category | flops | bytes accessed | tf_op | source)
XLA Modules:
  0.0 284.8 jit_solution(9534794592891662207)
XLA Ops:
  11.3 13.7 %all_to_all.27 = s32[8,3,5]{2,1,0:T(4,128)S(1)} all-to-all(s32[8,3,5]{2,1,0:T(4,128)S(1)} %reshape.243), channel_id=1, replica_groups=mesh['pair'=8,'occ'=4] {'pair'}, dimensions={0} | all-to-all | bytes 960 | tf_op jit(solution)/shard_map/all_to_all | solution.py:42
  25.1 1.7 gather_fusion.1
  28.3 4.4 %all-to-all-start.2 = ((f32[24,128,128]{2,1,0:T(8,128)}), f32[24,128,128]{2,1,0:T(8,128)}, u32[]{:S(2)}, u32[]{:S(2)}) async-start(f32[24,128,128]{2,1,0:T(8,128)} %select_multiply_fusion.1), calls=%async_computation.2 | async-start | bytes 3145728 | tf_op jit(solution)/shard_map/all_to_all | solution.py:67
  34.4 2.2 convolution_convert_fusion
  36.6 3.4 %reshape.175 = bf16[24,512,128]{2,1,0:T(8,128)(2,1)} reshape(bf16[96,16384]{1,0:T(8,128)(2,1)S(1)} %convolution_convert_fusion) | data formatting | bytes 6291456 | tf_op jit(solution)/shard_map/reshape | solution.py:53
  40.0 28.7 %all-to-all-done.2 = f32[24,128,128]{2,1,0:T(8,128)} async-done(((f32[24,128,128]{2,1,0:T(8,128)}), f32[24,128,128]{2,1,0:T(8,128)}, u32[]{:S(2)}, u32[]{:S(2)}) %all-to-all-start.2) | async-done | bytes 1572896 | tf_op jit(solution)/shard_map/all_to_all | solution.py:67
  68.7 3.6 %all-to-all-start.1 = ((bf16[24,512,128]{2,1,0:T(8,128)(2,1)}), bf16[24,512,128]{2,1,0:T(8,128)(2,1)S(1)}, u32[]{:S(2)}, u32[]{:S(2)}) async-start(bf16[24,512,128]{2,1,0:T(8,128)(2,1)} %reshape.175), calls=%async_computation.1 | async-start | bytes 6291456 | tf_op jit(solution)/shard_map/all_to_all | solution.py:54
  72.8 3.0 %gather_fusion.2 = f32[16,128,128]{2,1,0:T(8,128)} fusion(f32[24,128,128]{2,1,0:T(8,128)} %all-to-all-done.2, s32[1024]{0:T(1024)S(1)} %pad_clamp_fusion), kind=kCustom, calls=%fused_computation.1.clone | custom fusion | bytes 2097216 | tf_op jit(solution)/shard_map/jit(_take)/gather | solution.py:68
  75.8 2.4 broadcast_select_fusion.1
  78.2 64.8 %all-to-all-done.1 = bf16[24,512,128]{2,1,0:T(8,128)(2,1)S(1)} async-done(((bf16[24,512,128]{2,1,0:T(8,128)(2,1)}), bf16[24,512,128]{2,1,0:T(8,128)(2,1)S(1)}, u32[]{:S(2)}, u32[]{:S(2)}) %all-to-all-start.1) | async-done | bytes 3145760 | tf_op jit(solution)/shard_map/all_to_all | solution.py:54
  143.0 2.2 gather_fusion
  145.2 2.9 %copy.59 = bf16[16,512,128]{1,2,0:T(8,128)(2,1)S(1)} copy(bf16[16,512,128]{2,1,0:T(8,128)(2,1)} %gather_fusion) | data formatting | bytes 4194304 | tf_op jit(solution)/shard_map/jit(_take)/gather | solution.py:55
  148.0 2.1 fusion
  150.1 1.9 fusion.17
  153.2 4.7 %fusion.7 = f32[8,1,128,128]{3,1,2,0:T(1,128)} fusion(f32[8,2,1,1]{1,2,3,0:T(1,128)S(1)} %copy.65, f32[8,2,128,128]{3,2,1,0:T(8,128)S(1)} %fusion.18), kind=kOutput, calls=%fused_computation.16 | convolution fusion | flops 3145728 | bytes 1572928 | tf_op jit(solution)/shard_map/pc,pcae->pae/dot_general | solution.py:72
  158.0 20.7 %reduce-scatter.3.cloned.1.call-done = f32[8,32,128]{2,1,0:T(8,128)} async-done(((f32[8,128,128]{2,1,0:T(8,128)}), f32[8,32,128]{2,1,0:T(8,128)}) %reduce-scatter.3.cloned.1.call-update) | async-done | bytes 131088 | tf_op jit(solution)/shard_map/reduce_scatter | solution.py:73
  179.9 6.6 %all_gather.9 = f32[8,128,128]{2,1,0:T(8,128)S(1)} all-gather(f32[8,32,128]{2,1,0:T(8,128)S(1)} %divide_subtract_fusion.1), channel_id=1, replica_groups=mesh['pair'=8,'occ'=4] {'occ'}, dimensions={1}, use_global_device_ids=true | all-gather | bytes 655360 | tf_op jit(solution)/shard_map/all_gather | solution.py:82
  187.4 42.8 %all_to_all.28 = f32[24,128,128]{2,1,0:T(8,128)S(1)} all-to-all(f32[24,128,128]{2,1,0:T(8,128)S(1)} %select_multiply_fusion), channel_id=1, replica_groups=mesh['pair'=8,'occ'=4] {'pair'}, dimensions={0} | all-to-all | bytes 3145728 | tf_op jit(solution)/shard_map/all_to_all | solution.py:67
  230.2 1.6 gather_fusion.4
  233.2 1.8 fusion.19
  236.2 4.7 %fusion.5 = f32[8,1,128,128]{3,1,2,0:T(1,128)} fusion(f32[8,2,1,1]{1,2,3,0:T(1,128)S(1)} %copy.65, f32[8,2,128,128]{3,2,1,0:T(8,128)S(1)} %fusion.20), kind=kOutput, calls=%fused_computation.14 | convolution fusion | flops 3145728 | bytes 1572928 | tf_op jit(solution)/shard_map/pc,pcae->pae/dot_general | solution.py:72
  240.9 20.5 %reduce-scatter.5.cloned.1.call-done = f32[8,32,128]{2,1,0:T(8,128)} async-done(((f32[8,128,128]{2,1,0:T(8,128)}), f32[8,32,128]{2,1,0:T(8,128)}) %reduce-scatter.5.cloned.1.call-update) | async-done | bytes 131088 | tf_op jit(solution)/shard_map/reduce_scatter | solution.py:73
  262.5 6.6 %all_gather.10 = f32[8,128,128]{2,1,0:T(8,128)S(1)} all-gather(f32[8,32,128]{2,1,0:T(8,128)S(1)} %get-tuple-element.4), channel_id=1, replica_groups=mesh['pair'=8,'occ'=4] {'occ'}, dimensions={1}, use_global_device_ids=true | all-gather | bytes 655360 | tf_op jit(solution)/shard_map/all_gather | solution.py:82
  269.1 7.3 %all_gather.11 = f32[8,128,128]{2,1,0:T(8,128)S(1)} all-gather(f32[8,32,128]{2,1,0:T(8,128)S(1)} %get-tuple-element.5), channel_id=1, replica_groups=mesh['pair'=8,'occ'=4] {'occ'}, dimensions={1}, use_global_device_ids=true | all-gather | bytes 655360 | tf_op jit(solution)/shard_map/all_gather | solution.py:83
  (55 shorter events, 16.3 us)
Async XLA Ops:
  28.2 4.4 %copy-start.1 = (bf16[8,512,128]{2,1,0:T(8,128)(2,1)S(1)}, bf16[8,512,128]{2,1,0:T(8,128)(2,1)}, u32[]{:S(2)}) copy-start(bf16[8,512,128]{2,1,0:T(8,128)(2,1)} %param.17) | copy-start | bytes 3145732
  28.3 40.4 %all-to-all-start.2 = ((f32[24,128,128]{2,1,0:T(8,128)}), f32[24,128,128]{2,1,0:T(8,128)}, u32[]{:S(2)}, u32[]{:S(2)}) async-start(f32[24,128,128]{2,1,0:T(8,128)} %select_multiply_fusion.1), calls=%async_computation.2 | async-start | bytes 3145728 | tf_op jit(solution)/shard_map/all_to_all | solution.py:67
  40.0 32.4 %copy-start.4 = (f32[1,8,2]{1,2,0:T(2,128)S(1)}, f32[1,8,2]{1,2,0:T(2,128)}, u32[]{:S(2)}) copy-start(f32[1,8,2]{1,2,0:T(2,128)} %param.21) | copy-start | bytes 196
  68.7 74.3 %all-to-all-start.1 = ((bf16[24,512,128]{2,1,0:T(8,128)(2,1)}), bf16[24,512,128]{2,1,0:T(8,128)(2,1)S(1)}, u32[]{:S(2)}, u32[]{:S(2)}) async-start(bf16[24,512,128]{2,1,0:T(8,128)(2,1)} %reshape.175), calls=%async_computation.1 | async-start | bytes 6291456 | tf_op jit(solution)/shard_map/all_to_all | solution.py:54
  72.3 106.4 %reduce-scatter.3.cloned.1.call-start = ((), (), s32[]{:S(2)}) async-start(), calls=%async_computation.6 | async-start | bytes 655360 | tf_op jit(solution)/shard_map/reduce_scatter | solution.py:73
  148.0 2.1 copy-start
  153.2 4.8 %copy-start.2 = (f32[8,128]{1,0:T(8,128)S(1)}, f32[8,128]{1,0:T(8,128)}, u32[]{:S(2)}) copy-start(f32[8,128]{1,0:T(8,128)} %param.15) | copy-start | bytes 12292
  153.2 25.6 %copy-start.3 = (f32[8]{0:T(128)S(1)}, f32[8]{0:T(128)}, u32[]{:S(2)}) copy-start(f32[8]{0:T(128)} %param.16) | copy-start | bytes 100
  157.9 103.4 %reduce-scatter.5.cloned.1.call-start = ((), (), s32[]{:S(2)}) async-start(), calls=%async_computation.7 | async-start | bytes 655360 | tf_op jit(solution)/shard_map/reduce_scatter | solution.py:73
Sparse Core Ops, SparseCore 0:
  158.0 20.6 reduce-scatter.2
  241.0 20.2 reduce-scatter.4
where the time goes:
time: 286 us; the launch traced here: 285 us
  waiting for transfers between devices  135 us (47%)
  blocking collectives  76.9 us (27%)
  local copies, waits for them, and re-layouts  21.6 us (8%)
  matrix products  19.7 us (7%)
  between operations  14.3 us (5%)
  other arithmetic  9.41 us (3%)
  starting transfers between devices  8.15 us (3%)
    all_to_all x1, waiting for transfers between devices, local(): lax.all_to_all(moved_tiles, 'pair', split_axis=0, concat_axis=0, tiled=True)  64.8 us
    all_to_all x1, blocking collectives, local(): lax.all_to_all(packed, 'pair', split_axis=0, concat_axis=0, tiled=True)  42.8 us
    reduce_scatter x2, waiting for transfers between devices, local(): lax.psum_scatter(partial_value, 'occ', scatter_dimension=1, tiled=True)  41.2 us
    all_to_all x1, waiting for transfers between devices, local(): lax.all_to_all(packed, 'pair', split_axis=0, concat_axis=0, tiled=True)  28.7 us
    all_to_all x1, blocking collectives, local(): lax.all_to_all(requests, 'pair', split_axis=0, concat_axis=0, tiled=True)  13.7 us
    all_gather x2, blocking collectives, local(): lax.all_gather(updated_part, 'occ', axis=1, tiled=True)  13.2 us
    dot_general x2, matrix products, local(): jnp.einsum('pc,pcae->pae', weights, outer_prod, precision=HIGHEST)  9.38 us
    all_gather x1, blocking collectives, local(): lax.all_gather(residual_part, 'occ', axis=1, tiled=True)  7.26 us
  transfers between devices with their start and end apart: 4, of which 4 were waited for; matrix products, arithmetic and copies ran while one was open for 5% of the time, Pallas kernels for 0%

commit v1 on v0

v1 whole, which is shorter than its diff:
```python
import functools

import jax
import jax.numpy as jnp
import numpy as np
from jax import lax
from jax.experimental import pallas as pl
from jax.experimental.pallas import tpu as pltpu
from jax.sharding import PartitionSpec as P

ITERS = 2
UNROLL = 2
F32 = jnp.float32
BF16 = jnp.bfloat16
VMEM = pltpu.VMEM
SMEM = pltpu.SMEM


def ring_order(mesh):
    count = mesh.shape["pair"]
    try:
        spots = [tuple(d.coords)[1:3] for d in mesh.devices[:, 0]]
    except Exception:
        return list(range(count))
    ys = sorted({s[0] for s in spots})
    zs = sorted({s[1] for s in spots})
    where = {s: i for i, s in enumerate(spots)}
    if len(where) != count or len(ys) * len(zs) != count:
        return list(range(count))
    if len(zs) % 2 == 0:
        rows, cols, at = zs, ys, lambda r, c: (c, r)
    else:
        rows, cols, at = ys, zs, lambda r, c: (r, c)
    if len(rows) % 2 or len(cols) == 1:
        return list(range(count))
    walk = [at(rows[0], cols[0])]
    for i, r in enumerate(rows):
        inner = cols[1:] if i % 2 == 0 else cols[:0:-1]
        walk += [at(r, c) for c in inner]
    walk += [at(r, cols[0]) for r in rows[:0:-1]]
    return [where[s] for s in walk]


def ring_table(order):
    count = len(order)
    table = np.zeros((count, count), np.int32)
    for spot, device in enumerate(order):
        held = [device]
        for step in range(1, count // 2 + 1):
            held.append(order[(spot - step) % count])
            if len(held) < count:
                held.append(order[(spot + step) % count])
        table[device] = held[:count]
    return table


def ring_gather(order, own):
    count = len(order)
    right = [(order[i], order[(i + 1) % count]) for i in range(count)]
    left = [(b, a) for a, b in right]
    held = [own]
    ahead = behind = own
    for step in range(1, count // 2 + 1):
        ahead = lax.ppermute(ahead, "pair", right)
        held.append(ahead)
        if len(held) < count:
            behind = lax.ppermute(behind, "pair", left)
            held.append(behind)
    return held


def prep_kernel(per, tiles_ref, coef_ref, amp_ref, coef_out, amp_out, sem):
    first = lax.axis_index("occ") * per
    tiles = tiles_ref.shape[1]
    copies = [pltpu.make_async_copy(amp_ref.at[pl.ds(first, per)], amp_out, sem.at[per * tiles])]
    for i in range(per):
        for b in range(tiles):
            region = tiles_ref[first + i, b]
            copies.append(
                pltpu.make_async_copy(
                    coef_ref.at[first + i, b], coef_out.at[i, region], sem.at[i * tiles + b]
                )
            )
    for c in copies:
        c.start()
    for c in copies:
        c.wait()


def turn_kernel(tiles_ref, coef_ref, out_ref):
    pairs, tiles, size, width = coef_ref.shape
    for p in range(pairs):
        for b in range(tiles):
            at = pl.multiple_of(tiles_ref[p, b] * size, size)
            out_ref[p, :, pl.ds(at, size)] = coef_ref[p, b].T


def split(value):
    high = value.astype(BF16)
    low = (value - high.astype(F32)).astype(BF16)
    return high, low


def overlap_kernel(couples, table_ref, slot_ref, weight_ref, turned_ref, *refs):
    count = table_ref.shape[1]
    shards = refs[:count]
    s_out, pair_out, slot_out, weight_out, used_out, held, sem = refs[count:]
    me = lax.axis_index("pair")
    per = shards[0].shape[0]
    copies = []
    for k in range(count):
        at = table_ref[me, k] * per
        copies.append(pltpu.make_async_copy(shards[k], held.at[pl.ds(at, per)], sem.at[k]))
    for c in copies:
        c.start()

    def listing(j, used):
        slot = slot_ref[j]
        pair_out[used] = j // couples
        slot_out[used] = slot
        weight_out[used] = weight_ref[j]
        return used + jnp.where(slot >= 0, 1, 0)

    used = lax.fori_loop(0, slot_ref.shape[0], listing, 0)
    for k in range(UNROLL):
        pair_out[used + k] = 0
        slot_out[used + k] = 0
        weight_out[used + k] = 0.0
    used_out[0] = used
    for c in copies:
        c.wait()

    def step(g, carry):
        for k in range(UNROLL):
            i = g * UNROLL + k
            value = jnp.dot(turned_ref[pair_out[i]], held[slot_out[i]], preferred_element_type=F32)
            high, low = split(value)
            width = high.shape[1]
            s_out[i, :, :width] = high
            s_out[i, :, width:] = low
        return carry

    lax.fori_loop(0, (used + UNROLL - 1) // UNROLL, step, 0)


def couple_kernel(pairs, per, table_ref, pair_ref, slot_ref, weight_ref, used_ref, s_ref, *refs):
    count = table_ref.shape[1]
    shards = refs[:count]
    keep_out, send_out, held, cat, acc, sem = refs[count:]
    me = lax.axis_index("pair")
    occ = lax.axis_index("occ")
    occs = pairs // per
    copies = []
    for k in range(count):
        at = table_ref[me, k] * per
        copies.append(pltpu.make_async_copy(shards[k], held.at[pl.ds(at, per)], sem.at[k]))
    for c in copies:
        c.start()
    acc[...] = jnp.zeros_like(acc)
    width = held.shape[-1]
    for c in copies:
        c.wait()

    def halve(t, carry):
        high, low = split(held[t])
        cat[t, :width, :width] = high
        cat[t, width:, :width] = high
        cat[t, :width, width:] = low
        cat[t, width:, width:] = jnp.zeros_like(low)
        return carry

    lax.fori_loop(0, held.shape[0], halve, 0)

    def step(g, carry):
        for k in range(UNROLL):
            i = g * UNROLL + k
            p = pair_ref[i]
            both = s_ref[i]
            inner = jnp.dot(both, cat[slot_ref[i]], preferred_element_type=F32)
            inner = (inner[:, :width] + inner[:, width:]) * weight_ref[i]
            ih, il = split(inner)
            sh, sl = both[:, :width], both[:, width:]
            lhs = jnp.concatenate([ih, il], axis=1)
            rhs = jnp.concatenate(
                [
                    jnp.concatenate([sh, sh], axis=1),
                    jnp.concatenate([sl, jnp.zeros_like(sl)], axis=1),
                ],
                axis=0,
            )
            outer = lax.dot_general(
                lhs, rhs, (((1,), (1,)), ((), ())), preferred_element_type=F32
            )
            acc[p] += outer[:, :width] + outer[:, width:]
        return carry

    lax.fori_loop(0, (used_ref[0] + UNROLL - 1) // UNROLL, step, 0)
    half = occs // 2
    for away in range(half):
        chip = lax.rem(occ // 2 + away, half)
        core = lax.rem(occ, 2)
        keep_out[away] = acc[pl.ds((chip * 2 + core) * per, per)]
        send_out[away] = acc[pl.ds((chip * 2 + 1 - core) * per, per)]


def spec(space):
    return pl.BlockSpec(memory_space=space)


def local(
    order,
    amplitudes,
    exchange_ints,
    pno_energy,
    pair_shift,
    coefficients,
    domain_tiles,
    couple_owner,
    couple_index,
    couple_weight,
):
    pairs, width = amplitudes.shape[:2]
    domain = coefficients.shape[1]
    tiles = domain_tiles.shape[1]
    size = domain // tiles
    per_pair = couple_index.shape[2]
    count = lax.axis_size("pair")
    occs = lax.axis_size("occ")
    half = occs // 2
    per = pairs // occs
    occ = lax.axis_index("occ")
    total = occs * pairs * per_pair
    couples = occs * per_pair
    shape = jax.ShapeDtypeStruct
    table = jnp.asarray(ring_table(order))

    blocks = coefficients.reshape(pairs, tiles, size, width)
    own_coef, own_amp = pl.pallas_call(
        functools.partial(prep_kernel, per),
        out_shape=(shape((per, tiles, size, width), BF16), shape((per, width, width), F32)),
        in_specs=[spec(SMEM), spec(pl.ANY), spec(pl.ANY)],
        out_specs=(spec(VMEM), spec(VMEM)),
        scratch_shapes=[pltpu.SemaphoreType.DMA((per * tiles + 1,))],
        compiler_params=pltpu.CompilerParams(vmem_limit_bytes=8 << 20),
        name="prep",
    )(domain_tiles, blocks, amplitudes)
    own_coef = own_coef.reshape(per, domain, width)
    coef_held = ring_gather(order, own_coef)
    amp_held = ring_gather(order, own_amp)

    turned = pl.pallas_call(
        turn_kernel,
        out_shape=shape((pairs, width, domain), BF16),
        in_specs=[spec(SMEM), spec(VMEM)],
        out_specs=spec(VMEM),
        compiler_params=pltpu.CompilerParams(vmem_limit_bytes=8 << 20),
        name="turn",
    )(domain_tiles, blocks)

    partner = (couple_owner[..., 0] * pairs + couple_index).astype(F32)
    mine = jnp.stack([partner[0], couple_weight[0]])
    every = lax.all_gather(mine, "occ")
    every = jnp.transpose(every, (1, 2, 0, 3)).reshape(2, total)
    partner = every[0].astype(jnp.int32)
    place = partner % pairs - occ * per
    slots = jnp.where((place >= 0) & (place < per), partner // pairs * per + place, -1)
    room = total + UNROLL

    s_both, pair_list, slot_list, weight_list, used = pl.pallas_call(
        functools.partial(overlap_kernel, couples),
        out_shape=(
            shape((room, width, 2 * width), BF16),
            shape((room,), jnp.int32),
            shape((room,), jnp.int32),
            shape((room,), F32),
            shape((1,), jnp.int32),
        ),
        in_specs=[spec(SMEM)] * 3 + [spec(VMEM)] + [spec(pl.ANY)] * count,
        out_specs=(spec(VMEM),) + (spec(SMEM),) * 4,
        scratch_shapes=[
            VMEM((count * per, domain, width), BF16),
            pltpu.SemaphoreType.DMA((count,)),
        ],
        compiler_params=pltpu.CompilerParams(vmem_limit_bytes=48 << 20),
        name="overlap",
    )(table, slots, every[1], turned, *coef_held)

    def coupled(held):
        return pl.pallas_call(
            functools.partial(couple_kernel, pairs, per),
            out_shape=(shape((half, per, width, width), F32),) * 2,
            in_specs=[spec(SMEM)] * 5 + [spec(VMEM)] + [spec(pl.ANY)] * count,
            out_specs=(spec(VMEM),) * 2,
            scratch_shapes=[
                VMEM((count * per, width, width), F32),
                VMEM((count * per, 2 * width, 2 * width), BF16),
                VMEM((pairs, width, width), F32),
                pltpu.SemaphoreType.DMA((count,)),
            ],
            compiler_params=pltpu.CompilerParams(vmem_limit_bytes=52 << 20),
            name="couple",
        )(table, pair_list, slot_list, weight_list, used, s_both, *held)

    core_swap = [(o, o ^ 1) for o in range(occs)]

    def chip_shift(value, away):
        return lax.ppermute(
            value, "occ", [(o, (o + 2 * away) % occs) for o in range(occs)]
        )

    def quarter(value, first):
        return lax.dynamic_slice_in_dim(value, first * per, per, 0)

    def spread(energy, shift):
        return energy[:, :, None] + energy[:, None, :] + shift[:, None, None]

    def column(value):
        return jnp.stack([quarter(value, (occ + 2 * a) % occs) for a in range(half)])

    keep, send = coupled(amp_held)
    summed = keep + lax.ppermute(send, "occ", core_swap)
    part = summed[0]
    for away in range(1, half):
        part = part + chip_shift(summed[away], away)
    denominator = spread(quarter(pno_energy, occ), quarter(pair_shift, occ))
    residual = quarter(exchange_ints, occ) + denominator * own_amp - part
    current = own_amp - residual / denominator

    keep, send = coupled(ring_gather(order, current))
    summed = keep + lax.ppermute(send, "occ", core_swap)
    totals = summed
    for away in range(1, half):
        moved = chip_shift(summed, away)
        totals = totals + jnp.roll(moved, -away, axis=0)
    currents = jnp.stack(
        [current] + [chip_shift(current, half - away) for away in range(1, half)]
    )
    energies = column(pno_energy)
    shifts = column(pair_shift)
    denominators = (
        energies[:, :, :, None] + energies[:, :, None, :] + shifts[:, :, None, None]
    )
    residuals = column(exchange_ints) + denominators * currents - totals
    updates = currents - residuals / denominators
    mine = jnp.stack([updates, residuals])
    other = lax.ppermute(mine, "occ", core_swap)
    core = occ % 2
    even = jnp.where(core == 0, mine, other)
    odd = jnp.where(core == 0, other, mine)
    both = jnp.stack([even, odd], axis=2)
    both = jnp.roll(both, occ // 2, axis=1).reshape(2, pairs, width, width)
    return both[0], both[1]


def solution(mesh):
    in_specs = (
        P("pair", None, None),
        P("pair", None, None),
        P("pair", None),
        P("pair"),
        P("pair", None, None),
        P("pair", None),
        P("occ", "pair", None, None),
        P("occ", "pair", None),
        P("occ", "pair", None),
    )
    out_specs = (P("pair", None, None), P("pair", None, None))
    return jax.shard_map(
        functools.partial(local, ring_order(mesh)),
        mesh=mesh,
        in_specs=in_specs,
        out_specs=out_specs,
        check_vma=False,
    )
```

time: 286 us -> 119 us (0.42)
  waiting for transfers between devices: 135 us -> 44 us
  blocking collectives: 76.9 us -> 5.18 us
  starting transfers between devices: 8.15 us -> 34.2 us
  Pallas kernels: 0 us -> 20.8 us
  matrix products: 19.7 us -> 0 us
  between operations: 14.3 us -> 0.92 us
  local copies, waits for them, and re-layouts: 21.6 us -> 9.12 us
  other arithmetic: 9.41 us -> 2.76 us
    all_to_all x2 -> x0, waiting for transfers between devices: 93.5 us -> none  [the longest x1 64.8 us: local(): lax.all_to_all(moved_tiles, 'pair', split_axis=0, concat_axis=0, tiled=True)]
    all_to_all x2 -> x0, blocking collectives: 56.5 us -> none  [the longest x1 42.8 us: local(): lax.all_to_all(packed, 'pair', split_axis=0, concat_axis=0, tiled=True)]
    ppermute x0 -> x27, waiting for transfers between devices: none -> 44 us  [the longest x12 24.8 us: ring_gather(): ahead = lax.ppermute(ahead, 'pair', right)]
    reduce_scatter x2 -> x0, waiting for transfers between devices: 41.2 us -> none  [local(): lax.psum_scatter(partial_value, 'occ', scatter_dimension=1, tiled=True)]
    ppermute x0 -> x27, starting transfers between devices: none -> 34.2 us  [the longest x12 23 us: ring_gather(): ahead = lax.ppermute(ahead, 'pair', right)]
    pallas_call x0 -> x5, Pallas kernels: none -> 20.8 us  [the longest x2 13.6 us: coupled(): pl.pallas_call(functools.partial(couple_kernel, pairs, per), out_shape=(s...]
    dot_general x8 -> x0, matrix products: 19.7 us -> none  [the longest x2 9.38 us: local(): jnp.einsum('pc,pcae->pae', weights, outer_prod, precision=HIGHEST)]
    all_gather x3 -> x1, blocking collectives: 20.5 us -> 5.18 us  [local(): every = lax.all_gather(mine, 'occ')]
  transfers between devices with their start and end apart: 4 -> 27, of which waited for: 4 -> 14; matrix products, arithmetic and copies ran while one was open for 5% -> 5% of each run, Pallas kernels for 0% -> 5%
where the time goes in v1:
time: 119 us; the launch traced here: 117 us
  waiting for transfers between devices  44 us (37%)
  starting transfers between devices  34.2 us (29%)
  Pallas kernels  20.8 us (17%)
  local copies, waits for them, and re-layouts  9.12 us (8%)
  blocking collectives  5.18 us (4%)
  other arithmetic  2.76 us (2%)
    ppermute x12, waiting for transfers between devices, ring_gather(): ahead = lax.ppermute(ahead, 'pair', right)  24.8 us
    ppermute x12, starting transfers between devices, ring_gather(): ahead = lax.ppermute(ahead, 'pair', right)  23 us
    pallas_call x2, Pallas kernels, coupled(): pl.pallas_call(functools.partial(couple_kernel, pairs, per), out_shape=(s...  13.6 us
    ppermute x3, waiting for transfers between devices, chip_shift(): lax.ppermute(value, 'occ', [(o, (o + 2 * away) % occs) for o in range(occ...  13 us
    ppermute x3, starting transfers between devices, chip_shift(): lax.ppermute(value, 'occ', [(o, (o + 2 * away) % occs) for o in range(occ...  7.96 us
    all_gather x1, blocking collectives, local(): every = lax.all_gather(mine, 'occ')  5.18 us
    pallas_call x1, Pallas kernels, local(): pl.pallas_call(functools.partial(overlap_kernel, couples), out_shape=(sha...  5.02 us
    unnamed x17, local copies, waits for them, and re-layouts  3.71 us
  transfers between devices with their start and end apart: 27, of which 14 were waited for; matrix products, arithmetic and copies ran while one was open for 5% of the time, Pallas kernels for 5%

profile of v1, /device:TPU:0, one launch (start us, length us, event | category | flops | bytes accessed | tf_op | source)
XLA Modules:
  0.0 117.0 jit_solution(8060620316567929470)
XLA Ops:
  4.9 3.0 %collective-permute-start = (bf16[2,512,128]{2,1,0:T(8,128)(2,1)S(1)}, bf16[2,512,128]{2,1,0:T(8,128)(2,1)S(1)}, u32[]{:S(2)}, u32[]{:S(2)}) collective-permute-start(bf16[2,512,128]{2,1,0:T(8,128)(2,1)S(1)} %bitcast.46), channel_id=1, source_target_pairs={{0,4},{4,12},{12,20},{20,28},{28,24},{24,16},{16,8},{8,0},{1,5},{5... | collective-permute-start | bytes 786440 | tf_op jit(solution)/shard_map/ppermute | solution.py:64
  8.1 6.2 %collective-permute-done.refs_1_ = bf16[2,512,128]{2,1,0:T(8,128)(2,1)S(1)} collective-permute-done((bf16[2,512,128]{2,1,0:T(8,128)(2,1)S(1)}, bf16[2,512,128]{2,1,0:T(8,128)(2,1)S(1)}, u32[]{:S(2)}, u32[]{:S(2)}) %collective-permute-start) | collective-permute-done | bytes 262176 | tf_op jit(solution)/shard_map/ppermute | solution.py:64
  14.3 1.7 %collective-permute-start.2 = (bf16[2,512,128]{2,1,0:T(8,128)(2,1)S(1)}, bf16[2,512,128]{2,1,0:T(8,128)(2,1)S(1)}, u32[]{:S(2)}, u32[]{:S(2)}) collective-permute-start(bf16[2,512,128]{2,1,0:T(8,128)(2,1)S(1)} %collective-permute-done.refs_1_), channel_id=1, source_target_pairs={{0,4},{4,12},{12,20},{20,28},{28,24},{24,16},{16,8},{8,0},{1,5},{5... | collective-permute-start | bytes 786440 | tf_op jit(solution)/shard_map/ppermute | solution.py:64
  16.0 1.6 %collective-permute-start.7 = (f32[2,128,128]{2,1,0:T(8,128)S(1)}, f32[2,128,128]{2,1,0:T(8,128)S(1)}, u32[]{:S(2)}, u32[]{:S(2)}) collective-permute-start(f32[2,128,128]{2,1,0:T(8,128)S(1)} %get-tuple-element.13.refs_0_), channel_id=1, source_target_pairs={{0,4},{4,12},{12,20},{20,28},{28,24},{24,16},{16,8},{8,0},{1,5},{5... | collective-permute-start | bytes 393224 | tf_op jit(solution)/shard_map/ppermute | solution.py:64
  18.7 5.9 %collective-permute-done.7.refs_1_ = f32[2,128,128]{2,1,0:T(8,128)S(1)} collective-permute-done((f32[2,128,128]{2,1,0:T(8,128)S(1)}, f32[2,128,128]{2,1,0:T(8,128)S(1)}, u32[]{:S(2)}, u32[]{:S(2)}) %collective-permute-start.7) | collective-permute-done | bytes 131104 | tf_op jit(solution)/shard_map/ppermute | solution.py:64
  29.4 5.2 %all-gather = f32[8,8,2]{1,2,0:T(2,128)S(1)} all-gather(f32[2,8,2]{1,2,0:T(2,128)S(1)} %pad_maximum_fusion.2), channel_id=2, replica_groups=mesh['pair'=8,'occ'=4] {'occ'}, dimensions={0}, use_global_device_ids=true | all-gather | bytes 640 | tf_op jit(solution)/shard_map/all_gather | solution.py:262
  48.1 5.0 %overlap.1 = (bf16[66,128,256]{2,1,0:T(8,128)(2,1)}, s32[66]{0:T(128)S(1)}, s32[66]{0:T(128)S(1)}, f32[66]{0:T(128)S(1)}, s32[1]{0:T(128)}) custom-call(s32[8,8]{1,0:T(8,128)S(1)} %copy-done.3, s32[64]{0:T(128)S(1)} %and_select_fusion.1.slot_ref, f32[64]{0:T(128)S(1)} %copy-done.4, bf16[8,128,512]{2,1,0:T(8,128)(2,1)S(1)} %turn.1.turned_ref, ...), custom_call_target="tpu_custom_call" | custom-call | tf_op jit(solution)/shard_map/overlap/pallas_call | solution.py:269
  53.1 6.9 %couple.2 = (f32[2,2,128,128]{3,2,1,0:T(8,128)S(1)}, f32[2,2,128,128]{3,2,1,0:T(8,128)S(1)}) custom-call(s32[8,8]{1,0:T(8,128)S(1)} %copy-done.3, s32[66]{0:T(128)S(1)} %get-tuple-element.15.pair_ref, s32[66]{0:T(128)S(1)} %get-tuple-element.16.slot_ref, f32[66]{0:T(128)S(1)} %get-tuple-element.17.weight_ref, s32[1]{0:T(128)} %get-tuple-element.18.used_ref, ...), custom_call_target="tpu_custom_call" | custom-call | tf_op jit(solution)/shard_map/couple/pallas_call | solution.py:289
  61.7 4.3 %collective-permute-start.15 = (f32[2,128,128]{2,1,0:T(8,128)S(1)}, f32[2,128,128]{2,1,0:T(8,128)S(1)}, u32[]{:S(2)}, u32[]{:S(2)}) collective-permute-start(f32[2,128,128]{2,1,0:T(8,128)S(1)} %slice_bitcast_fusion), channel_id=1, source_target_pairs={{0,2},{1,3},{2,0},{3,1},{4,6},{5,7},{6,4},{7,5},{8,10},{9,11},{10,... | collective-permute-start | bytes 393224 | tf_op jit(solution)/shard_map/ppermute | solution.py:307
  66.1 3.7 %collective-permute-done.15 = f32[2,128,128]{2,1,0:T(8,128)S(1)} collective-permute-done((f32[2,128,128]{2,1,0:T(8,128)S(1)}, f32[2,128,128]{2,1,0:T(8,128)S(1)}, u32[]{:S(2)}, u32[]{:S(2)}) %collective-permute-start.15) | collective-permute-done | bytes 131104 | tf_op jit(solution)/shard_map/ppermute | solution.py:307
  69.9 2.4 %collective-permute-start.17 = (f32[2,128,128]{2,1,0:T(8,128)S(1)}, f32[2,128,128]{2,1,0:T(8,128)S(1)}, u32[]{:S(2)}, u32[]{:S(2)}) collective-permute-start(f32[2,128,128]{2,1,0:T(8,128)S(1)} %get-tuple-element.31.refs_0_), channel_id=1, source_target_pairs={{0,4},{4,12},{12,20},{20,28},{28,24},{24,16},{16,8},{8,0},{1,5},{5... | collective-permute-start | bytes 393224 | tf_op jit(solution)/shard_map/ppermute | solution.py:64
  72.3 2.6 %collective-permute-done.17.refs_1_ = f32[2,128,128]{2,1,0:T(8,128)S(1)} collective-permute-done((f32[2,128,128]{2,1,0:T(8,128)S(1)}, f32[2,128,128]{2,1,0:T(8,128)S(1)}, u32[]{:S(2)}, u32[]{:S(2)}) %collective-permute-start.17) | collective-permute-done | bytes 131104 | tf_op jit(solution)/shard_map/ppermute | solution.py:64
  75.0 2.3 %collective-permute-start.19 = (f32[2,128,128]{2,1,0:T(8,128)S(1)}, f32[2,128,128]{2,1,0:T(8,128)S(1)}, u32[]{:S(2)}, u32[]{:S(2)}) collective-permute-start(f32[2,128,128]{2,1,0:T(8,128)S(1)} %collective-permute-done.17.refs_1_), channel_id=1, source_target_pairs={{0,4},{4,12},{12,20},{20,28},{28,24},{24,16},{16,8},{8,0},{1,5},{5... | collective-permute-start | bytes 393224 | tf_op jit(solution)/shard_map/ppermute | solution.py:64
  77.3 2.9 %collective-permute-done.19.refs_3_ = f32[2,128,128]{2,1,0:T(8,128)S(1)} collective-permute-done((f32[2,128,128]{2,1,0:T(8,128)S(1)}, f32[2,128,128]{2,1,0:T(8,128)S(1)}, u32[]{:S(2)}, u32[]{:S(2)}) %collective-permute-start.19) | collective-permute-done | bytes 131104 | tf_op jit(solution)/shard_map/ppermute | solution.py:64
  80.2 2.5 %collective-permute-start.21 = (f32[2,128,128]{2,1,0:T(8,128)S(1)}, f32[2,128,128]{2,1,0:T(8,128)S(1)}, u32[]{:S(2)}, u32[]{:S(2)}) collective-permute-start(f32[2,128,128]{2,1,0:T(8,128)S(1)} %collective-permute-done.19.refs_3_), channel_id=1, source_target_pairs={{0,4},{4,12},{12,20},{20,28},{28,24},{24,16},{16,8},{8,0},{1,5},{5... | collective-permute-start | bytes 393224 | tf_op jit(solution)/shard_map/ppermute | solution.py:64
  82.7 3.7 %collective-permute-done.21.refs_5_ = f32[2,128,128]{2,1,0:T(8,128)S(1)} collective-permute-done((f32[2,128,128]{2,1,0:T(8,128)S(1)}, f32[2,128,128]{2,1,0:T(8,128)S(1)}, u32[]{:S(2)}, u32[]{:S(2)}) %collective-permute-start.21) | collective-permute-done | bytes 131104 | tf_op jit(solution)/shard_map/ppermute | solution.py:64
  86.4 2.5 %collective-permute-start.23 = (f32[2,128,128]{2,1,0:T(8,128)S(1)}, f32[2,128,128]{2,1,0:T(8,128)S(1)}, u32[]{:S(2)}, u32[]{:S(2)}) collective-permute-start(f32[2,128,128]{2,1,0:T(8,128)S(1)} %collective-permute-done.21.refs_5_), channel_id=1, source_target_pairs={{0,4},{4,12},{12,20},{20,28},{28,24},{24,16},{16,8},{8,0},{1,5},{5... | collective-permute-start | bytes 393224 | tf_op jit(solution)/shard_map/ppermute | solution.py:64
  88.9 2.5 %collective-permute-done.23.refs_7_ = f32[2,128,128]{2,1,0:T(8,128)S(1)} collective-permute-done((f32[2,128,128]{2,1,0:T(8,128)S(1)}, f32[2,128,128]{2,1,0:T(8,128)S(1)}, u32[]{:S(2)}, u32[]{:S(2)}) %collective-permute-start.23) | collective-permute-done | bytes 131104 | tf_op jit(solution)/shard_map/ppermute | solution.py:64
  91.4 6.7 %couple.3 = (f32[2,2,128,128]{3,2,1,0:T(8,128)S(1)}, f32[2,2,128,128]{3,2,1,0:T(8,128)S(1)}) custom-call(s32[8,8]{1,0:T(8,128)S(1)} %copy-done.3, s32[66]{0:T(128)S(1)} %get-tuple-element.15.pair_ref, s32[66]{0:T(128)S(1)} %get-tuple-element.16.slot_ref, f32[66]{0:T(128)S(1)} %get-tuple-element.17.weight_ref, s32[1]{0:T(128)} %get-tuple-element.18.used_ref, ...), custom_call_target="tpu_custom_call" | custom-call | tf_op jit(solution)/shard_map/couple/pallas_call | solution.py:289
  98.2 1.5 %collective-permute-done.24 = f32[2,2,128,128]{3,2,1,0:T(8,128)S(1)} collective-permute-done((f32[2,2,128,128]{3,2,1,0:T(8,128)S(1)}, f32[2,2,128,128]{3,2,1,0:T(8,128)S(1)}, u32[]{:S(2)}, u32[]{:S(2)}) %collective-permute-start.24) | collective-permute-done | bytes 262176 | tf_op jit(solution)/shard_map/ppermute | solution.py:330
  99.8 3.6 %collective-permute-start.25 = (f32[2,2,128,128]{3,2,1,0:T(8,128)S(1)}, f32[2,2,128,128]{3,2,1,0:T(8,128)S(1)}, u32[]{:S(2)}, u32[]{:S(2)}) collective-permute-start(f32[2,2,128,128]{3,2,1,0:T(8,128)S(1)} %add.142), channel_id=1, source_target_pairs={{0,2},{1,3},{2,0},{3,1},{4,6},{5,7},{6,4},{7,5},{8,10},{9,11},{10,... | collective-permute-start | bytes 786440 | tf_op jit(solution)/shard_map/ppermute | solution.py:307
  103.5 7.0 %collective-permute-done.25 = f32[2,2,128,128]{3,2,1,0:T(8,128)S(1)} collective-permute-done((f32[2,2,128,128]{3,2,1,0:T(8,128)S(1)}, f32[2,2,128,128]{3,2,1,0:T(8,128)S(1)}, u32[]{:S(2)}, u32[]{:S(2)}) %collective-permute-start.25) | collective-permute-done | bytes 262176 | tf_op jit(solution)/shard_map/ppermute | solution.py:307
  110.5 2.2 %collective-permute-done.16 = f32[2,128,128]{2,1,0:T(8,128)S(1)} collective-permute-done((f32[2,128,128]{2,1,0:T(8,128)S(1)}, f32[2,128,128]{2,1,0:T(8,128)S(1)}, u32[]{:S(2)}, u32[]{:S(2)}) %collective-permute-start.16) | collective-permute-done | bytes 131104 | tf_op jit(solution)/shard_map/ppermute | solution.py:307
  113.1 1.9 %collective-permute-done.26 = f32[2,2,2,128,128]{4,3,2,1,0:T(8,128)S(1)} collective-permute-done((f32[2,2,2,128,128]{4,3,2,1,0:T(8,128)S(1)}, f32[2,2,2,128,128]{4,3,2,1,0:T(8,128)S(1)}, u32[]{:S(2)}, u32[]{:S(2)}) %collective-permute-start.26) | collective-permute-done | bytes 524320 | tf_op jit(solution)/shard_map/ppermute | solution.py:346
  (79 shorter events, 28.1 us)
Async XLA Ops:
  4.9 9.4 %collective-permute-start = (bf16[2,512,128]{2,1,0:T(8,128)(2,1)S(1)}, bf16[2,512,128]{2,1,0:T(8,128)(2,1)S(1)}, u32[]{:S(2)}, u32[]{:S(2)}) collective-permute-start(bf16[2,512,128]{2,1,0:T(8,128)(2,1)S(1)} %bitcast.46), channel_id=1, source_target_pairs={{0,4},{4,12},{12,20},{20,28},{28,24},{24,16},{16,8},{8,0},{1,5},{5... | collective-permute-start | bytes 786440 | tf_op jit(solution)/shard_map/ppermute | solution.py:64
  7.9 18.0 %collective-permute-start.1 = (bf16[2,512,128]{2,1,0:T(8,128)(2,1)S(1)}, bf16[2,512,128]{2,1,0:T(8,128)(2,1)S(1)}, u32[]{:S(2)}, u32[]{:S(2)}) collective-permute-start(bf16[2,512,128]{2,1,0:T(8,128)(2,1)S(1)} %bitcast.47), channel_id=1, source_target_pairs={{4,0},{12,4},{20,12},{28,20},{24,28},{16,24},{8,16},{0,8},{5,1},{1... | collective-permute-start | bytes 786440 | tf_op jit(solution)/shard_map/ppermute | solution.py:67
  14.3 12.3 %collective-permute-start.2 = (bf16[2,512,128]{2,1,0:T(8,128)(2,1)S(1)}, bf16[2,512,128]{2,1,0:T(8,128)(2,1)S(1)}, u32[]{:S(2)}, u32[]{:S(2)}) collective-permute-start(bf16[2,512,128]{2,1,0:T(8,128)(2,1)S(1)} %collective-permute-done.refs_1_), channel_id=1, source_target_pairs={{0,4},{4,12},{12,20},{20,28},{28,24},{24,16},{16,8},{8,0},{1,5},{5... | collective-permute-start | bytes 786440 | tf_op jit(solution)/shard_map/ppermute | solution.py:64
  16.0 8.6 %collective-permute-start.7 = (f32[2,128,128]{2,1,0:T(8,128)S(1)}, f32[2,128,128]{2,1,0:T(8,128)S(1)}, u32[]{:S(2)}, u32[]{:S(2)}) collective-permute-start(f32[2,128,128]{2,1,0:T(8,128)S(1)} %get-tuple-element.13.refs_0_), channel_id=1, source_target_pairs={{0,4},{4,12},{12,20},{20,28},{28,24},{24,16},{16,8},{8,0},{1,5},{5... | collective-permute-start | bytes 393224 | tf_op jit(solution)/shard_map/ppermute | solution.py:64
  17.6 17.0 %collective-permute-start.8 = (f32[2,128,128]{2,1,0:T(8,128)S(1)}, f32[2,128,128]{2,1,0:T(8,128)S(1)}, u32[]{:S(2)}, u32[]{:S(2)}) collective-permute-start(f32[2,128,128]{2,1,0:T(8,128)S(1)} %get-tuple-element.13.refs_0_), channel_id=1, source_target_pairs={{4,0},{12,4},{20,12},{28,20},{24,28},{16,24},{8,16},{0,8},{5,1},{1... | collective-permute-start | bytes 393224 | tf_op jit(solution)/shard_map/ppermute | solution.py:67
  24.6 10.6 %collective-permute-start.9 = (f32[2,128,128]{2,1,0:T(8,128)S(1)}, f32[2,128,128]{2,1,0:T(8,128)}, u32[]{:S(2)}, u32[]{:S(2)}) collective-permute-start(f32[2,128,128]{2,1,0:T(8,128)S(1)} %collective-permute-done.7.refs_1_), channel_id=1, source_target_pairs={{0,4},{4,12},{12,20},{20,28},{28,24},{24,16},{16,8},{8,0},{1,5},{5... | collective-permute-start | bytes 393224 | tf_op jit(solution)/shard_map/ppermute | solution.py:64
  26.0 10.6 %collective-permute-start.3 = (bf16[2,512,128]{2,1,0:T(8,128)(2,1)S(1)}, bf16[2,512,128]{2,1,0:T(8,128)(2,1)S(1)}, u32[]{:S(2)}, u32[]{:S(2)}) collective-permute-start(bf16[2,512,128]{2,1,0:T(8,128)(2,1)S(1)} %collective-permute-done.1.refs_2_), channel_id=1, source_target_pairs={{4,0},{12,4},{20,12},{28,20},{24,28},{16,24},{8,16},{0,8},{5,1},{1... | collective-permute-start | bytes 786440 | tf_op jit(solution)/shard_map/ppermute | solution.py:67
  26.6 10.6 %collective-permute-start.4 = (bf16[2,512,128]{2,1,0:T(8,128)(2,1)S(1)}, bf16[2,512,128]{2,1,0:T(8,128)(2,1)S(1)}, u32[]{:S(2)}, u32[]{:S(2)}) collective-permute-start(bf16[2,512,128]{2,1,0:T(8,128)(2,1)S(1)} %collective-permute-done.2.refs_3_), channel_id=1, source_target_pairs={{0,4},{4,12},{12,20},{20,28},{28,24},{24,16},{16,8},{8,0},{1,5},{5... | collective-permute-start | bytes 786440 | tf_op jit(solution)/shard_map/ppermute | solution.py:64
  34.6 8.6 %collective-permute-start.10 = (f32[2,128,128]{2,1,0:T(8,128)S(1)}, f32[2,128,128]{2,1,0:T(8,128)}, u32[]{:S(2)}, u32[]{:S(2)}) collective-permute-start(f32[2,128,128]{2,1,0:T(8,128)S(1)} %collective-permute-done.8.refs_2_), channel_id=1, source_target_pairs={{4,0},{12,4},{20,12},{28,20},{24,28},{16,24},{8,16},{0,8},{5,1},{1... | collective-permute-start | bytes 393224 | tf_op jit(solution)/shard_map/ppermute | solution.py:67
  35.2 8.6 %collective-permute-start.11 = (f32[2,128,128]{2,1,0:T(8,128)}, f32[2,128,128]{2,1,0:T(8,128)}, u32[]{:S(2)}, u32[]{:S(2)}) collective-permute-start(f32[2,128,128]{2,1,0:T(8,128)} %collective-permute-done.9.refs_3_), channel_id=1, source_target_pairs={{0,4},{4,12},{12,20},{20,28},{28,24},{24,16},{16,8},{8,0},{1,5},{5... | collective-permute-start | bytes 393224 | tf_op jit(solution)/shard_map/ppermute | solution.py:64
  36.6 10.0 %collective-permute-start.5 = (bf16[2,512,128]{2,1,0:T(8,128)(2,1)S(1)}, bf16[2,512,128]{2,1,0:T(8,128)(2,1)S(1)}, u32[]{:S(2)}, u32[]{:S(2)}) collective-permute-start(bf16[2,512,128]{2,1,0:T(8,128)(2,1)S(1)} %collective-permute-done.3.refs_4_), channel_id=1, source_target_pairs={{4,0},{12,4},{20,12},{28,20},{24,28},{16,24},{8,16},{0,8},{5,1},{1... | collective-permute-start | bytes 786440 | tf_op jit(solution)/shard_map/ppermute | solution.py:67
  37.2 10.2 %collective-permute-start.6 = (bf16[2,512,128]{2,1,0:T(8,128)(2,1)S(1)}, bf16[2,512,128]{2,1,0:T(8,128)(2,1)S(1)}, u32[]{:S(2)}, u32[]{:S(2)}) collective-permute-start(bf16[2,512,128]{2,1,0:T(8,128)(2,1)S(1)} %collective-permute-done.4.refs_5_), channel_id=1, source_target_pairs={{0,4},{4,12},{12,20},{20,28},{28,24},{24,16},{16,8},{8,0},{1,5},{5... | collective-permute-start | bytes 786440 | tf_op jit(solution)/shard_map/ppermute | solution.py:64
  43.2 9.9 %collective-permute-start.12 = (f32[2,128,128]{2,1,0:T(8,128)}, f32[2,128,128]{2,1,0:T(8,128)S(1)}, u32[]{:S(2)}, u32[]{:S(2)}) collective-permute-start(f32[2,128,128]{2,1,0:T(8,128)} %collective-permute-done.10.refs_4_), channel_id=1, source_target_pairs={{4,0},{12,4},{20,12},{28,20},{24,28},{16,24},{8,16},{0,8},{5,1},{1... | collective-permute-start | bytes 393224 | tf_op jit(solution)/shard_map/ppermute | solution.py:67
  43.8 9.3 %collective-permute-start.13 = (f32[2,128,128]{2,1,0:T(8,128)}, f32[2,128,128]{2,1,0:T(8,128)S(1)}, u32[]{:S(2)}, u32[]{:S(2)}) collective-permute-start(f32[2,128,128]{2,1,0:T(8,128)} %collective-permute-done.11.refs_5_), channel_id=1, source_target_pairs={{0,4},{4,12},{12,20},{20,28},{28,24},{24,16},{16,8},{8,0},{1,5},{5... | collective-permute-start | bytes 393224 | tf_op jit(solution)/shard_map/ppermute | solution.py:64
  61.7 8.1 %collective-permute-start.15 = (f32[2,128,128]{2,1,0:T(8,128)S(1)}, f32[2,128,128]{2,1,0:T(8,128)S(1)}, u32[]{:S(2)}, u32[]{:S(2)}) collective-permute-start(f32[2,128,128]{2,1,0:T(8,128)S(1)} %slice_bitcast_fusion), channel_id=1, source_target_pairs={{0,2},{1,3},{2,0},{3,1},{4,6},{5,7},{6,4},{7,5},{8,10},{9,11},{10,... | collective-permute-start | bytes 393224 | tf_op jit(solution)/shard_map/ppermute | solution.py:307
  69.9 5.0 %collective-permute-start.17 = (f32[2,128,128]{2,1,0:T(8,128)S(1)}, f32[2,128,128]{2,1,0:T(8,128)S(1)}, u32[]{:S(2)}, u32[]{:S(2)}) collective-permute-start(f32[2,128,128]{2,1,0:T(8,128)S(1)} %get-tuple-element.31.refs_0_), channel_id=1, source_target_pairs={{0,4},{4,12},{12,20},{20,28},{28,24},{24,16},{16,8},{8,0},{1,5},{5... | collective-permute-start | bytes 393224 | tf_op jit(solution)/shard_map/ppermute | solution.py:64
  72.3 5.0 %collective-permute-start.18 = (f32[2,128,128]{2,1,0:T(8,128)S(1)}, f32[2,128,128]{2,1,0:T(8,128)S(1)}, u32[]{:S(2)}, u32[]{:S(2)}) collective-permute-start(f32[2,128,128]{2,1,0:T(8,128)S(1)} %get-tuple-element.31.refs_0_), channel_id=1, source_target_pairs={{4,0},{12,4},{20,12},{28,20},{24,28},{16,24},{8,16},{0,8},{5,1},{1... | collective-permute-start | bytes 393224 | tf_op jit(solution)/shard_map/ppermute | solution.py:67
  75.0 5.2 %collective-permute-start.19 = (f32[2,128,128]{2,1,0:T(8,128)S(1)}, f32[2,128,128]{2,1,0:T(8,128)S(1)}, u32[]{:S(2)}, u32[]{:S(2)}) collective-permute-start(f32[2,128,128]{2,1,0:T(8,128)S(1)} %collective-permute-done.17.refs_1_), channel_id=1, source_target_pairs={{0,4},{4,12},{12,20},{20,28},{28,24},{24,16},{16,8},{8,0},{1,5},{5... | collective-permute-start | bytes 393224 | tf_op jit(solution)/shard_map/ppermute | solution.py:64
  77.3 5.4 %collective-permute-start.20 = (f32[2,128,128]{2,1,0:T(8,128)S(1)}, f32[2,128,128]{2,1,0:T(8,128)S(1)}, u32[]{:S(2)}, u32[]{:S(2)}) collective-permute-start(f32[2,128,128]{2,1,0:T(8,128)S(1)} %collective-permute-done.18.refs_2_), channel_id=1, source_target_pairs={{4,0},{12,4},{20,12},{28,20},{24,28},{16,24},{8,16},{0,8},{5,1},{1... | collective-permute-start | bytes 393224 | tf_op jit(solution)/shard_map/ppermute | solution.py:67
  80.2 6.2 %collective-permute-start.21 = (f32[2,128,128]{2,1,0:T(8,128)S(1)}, f32[2,128,128]{2,1,0:T(8,128)S(1)}, u32[]{:S(2)}, u32[]{:S(2)}) collective-permute-start(f32[2,128,128]{2,1,0:T(8,128)S(1)} %collective-permute-done.19.refs_3_), channel_id=1, source_target_pairs={{0,4},{4,12},{12,20},{20,28},{28,24},{24,16},{16,8},{8,0},{1,5},{5... | collective-permute-start | bytes 393224 | tf_op jit(solution)/shard_map/ppermute | solution.py:64
  82.7 6.2 %collective-permute-start.22 = (f32[2,128,128]{2,1,0:T(8,128)S(1)}, f32[2,128,128]{2,1,0:T(8,128)S(1)}, u32[]{:S(2)}, u32[]{:S(2)}) collective-permute-start(f32[2,128,128]{2,1,0:T(8,128)S(1)} %collective-permute-done.20.refs_4_), channel_id=1, source_target_pairs={{4,0},{12,4},{20,12},{28,20},{24,28},{16,24},{8,16},{0,8},{5,1},{1... | collective-permute-start | bytes 393224 | tf_op jit(solution)/shard_map/ppermute | solution.py:67
  86.4 5.0 %collective-permute-start.23 = (f32[2,128,128]{2,1,0:T(8,128)S(1)}, f32[2,128,128]{2,1,0:T(8,128)S(1)}, u32[]{:S(2)}, u32[]{:S(2)}) collective-permute-start(f32[2,128,128]{2,1,0:T(8,128)S(1)} %collective-permute-done.21.refs_5_), channel_id=1, source_target_pairs={{0,4},{4,12},{12,20},{20,28},{28,24},{24,16},{16,8},{8,0},{1,5},{5... | collective-permute-start | bytes 393224 | tf_op jit(solution)/shard_map/ppermute | solution.py:64
  99.8 10.8 %collective-permute-start.25 = (f32[2,2,128,128]{3,2,1,0:T(8,128)S(1)}, f32[2,2,128,128]{3,2,1,0:T(8,128)S(1)}, u32[]{:S(2)}, u32[]{:S(2)}) collective-permute-start(f32[2,2,128,128]{3,2,1,0:T(8,128)S(1)} %add.142), channel_id=1, source_target_pairs={{0,2},{1,3},{2,0},{3,1},{4,6},{5,7},{6,4},{7,5},{8,10},{9,11},{10,... | collective-permute-start | bytes 786440 | tf_op jit(solution)/shard_map/ppermute | solution.py:307
  103.4 9.4 %collective-permute-start.16 = (f32[2,128,128]{2,1,0:T(8,128)S(1)}, f32[2,128,128]{2,1,0:T(8,128)S(1)}, u32[]{:S(2)}, u32[]{:S(2)}) collective-permute-start(f32[2,128,128]{2,1,0:T(8,128)S(1)} %get-tuple-element.31.refs_0_), channel_id=1, source_target_pairs={{0,2},{1,3},{2,0},{3,1},{4,6},{5,7},{6,4},{7,5},{8,10},{9,11},{10,... | collective-permute-start | bytes 393224 | tf_op jit(solution)/shard_map/ppermute | solution.py:307
  (11 other events, 132.3 us)
